TPU v7x, 256 devices: a 4x2x16 block of a 4x16x16 slice. The times are simulated.
256 devices in a mesh: groups: 2 (over y), dp: 16 (over z), section: 4 (over x), tensor: 2 (over core).
Axes of the slice: x: 4, y: 2, z: 16, core: 2. Of those that a mesh axis runs over, the one named last changes fastest.
The devices are a block of a 4x16x16 slice.
Arguments:
- hidden: bfloat16 [512, 8, 5120], P(('groups', 'dp')), parts along dimension 0, may hold values from -6 to 6
- unembed: bfloat16 [512, 8, 5120], P(('groups', 'dp')), parts along dimension 0, may hold values from -0.02734375 to 0.02734375
- value_proj: bfloat16 [4, 5120, 512], P('section', 'dp', 'tensor'), may hold values from -0.078125 to 0.078125
- output_proj: bfloat16 [4, 512, 5120], P('section', 'tensor', 'dp'), may hold values from -0.125 to 0.125
- norm_gains: float32 [4, 5120], P('section'), may hold values from 0.1 to 1.9
- survive: int32 [32], P(('groups', 'dp')), parts along dimension 0, may hold values from 0 to 1, as said below
- lengths: int32 [512], P(('groups', 'dp')), parts along dimension 0, may hold values from 1 to 8
- assign: int32 [512], P(('groups', 'dp')), parts along dimension 0, may hold values from 0 to 16, as said below
- advantage: float32 [512], P(('groups', 'dp')), parts along dimension 0, may hold values from -4 to 4
- reference_logit: float32 [512, 8], P(('groups', 'dp')), parts along dimension 0, may hold values from -4 to 4
- recorded_gap: float32 [512, 8], P(('groups', 'dp')), parts along dimension 0, may hold values from -2 to 2
Outputs:
- grad_value: float32 [8, 5120, 512], P(('groups', 'section'), 'dp', 'tensor'), parts along dimension 0
- grad_output: float32 [8, 512, 5120], P(('groups', 'section'), 'tensor', 'dp'), parts along dimension 0
There are 2 independent parts, one for each index of `groups`. A program takes and returns all parts, laid end to end along the dimension named above; an argument that names none is the same for every part. Nothing has to cross between parts.
Inputs may be any that keep to these rules, and one draw needn't show every extreme that they name: `survive`: 1 where the group of 16 responses is kept, 0 where it is dropped; in every draw all groups of some dp index are kept. `assign`: the 16 slots of a dp index list the local positions (0 to 15) of the responses of its kept groups, each exactly once, then hold 16 in every other slot.
All inputs are finite; a program needn't handle non-finite values.
Results may differ from a plain program's by a relative error of at most 0.029.
Values may be sent and summed in bfloat16 or wider, within the bound.
A program may use at most 64 MiB of HBM per device.

v0:
```python
import math
import jax
import jax.numpy as jnp
from jax import lax
from jax.sharding import PartitionSpec as P

GROUP = 16
MB_RESP = 8
eps_norm = 1e-06
loss_scale = 4096.0
clip_high = math.log(1.28)
clip_low = math.log(0.8)


def turned_gather(arrays, axis, dims):
    turned = [jnp.moveaxis(a, dim, 0) for a, dim in zip(arrays, dims)]
    widths = [t[0].size for t in turned]
    both = jnp.concatenate([t.reshape(-1, w) for t, w in zip(turned, widths)], axis=1)
    result = lax.all_gather(both, axis, axis=0, tiled=True)
    tiles = jnp.split(result, [sum(widths[:k]) for k in range(1, len(widths))], axis=1)
    return tuple(
        (
            jnp.moveaxis(b.reshape(-1, *t.shape[1:]), 0, dim)
            for b, t, dim in zip(tiles, turned, dims)
        )
    )


def copy_for_each(array, axis):
    devices = lax.axis_size(axis)
    return lax.all_to_all(
        jnp.broadcast_to(array[None], (devices, *array.shape)), axis, 0, 0, tiled=True
    )


def taken_together(array, axis):
    return copy_for_each(array, axis).astype(jnp.float32).sum(axis=0)


def from_behind(block, axis, distance):
    devices = range(lax.axis_size(axis))
    route = [(i - distance, i) for i in devices if i - distance in devices]
    return lax.ppermute(block, axis, route)


def of_everyone(array, axis):
    everything = copy_for_each(array, axis)
    return jnp.sum(everything, axis=0)


def norm_forward(row_block, norm_gain):
    values = row_block.astype(jnp.float32)
    inverse = lax.rsqrt(jnp.mean(values * values, axis=-1, keepdims=True) + eps_norm)
    return (values, inverse, (values * inverse * norm_gain).astype(jnp.bfloat16))


def norm_backward(values, inverse, norm_gain, upstream):
    scaled = upstream * norm_gain
    inner_sum = jnp.sum(scaled * values, axis=-1, keepdims=True) / values.shape[-1]
    return inverse * scaled - values * (inverse * inverse * inverse) * inner_sum


def contract_last(left_rows, right_rows):
    return lax.dot_general(
        left_rows, right_rows, (((1,), (1,)), ((), ())), preferred_element_type=jnp.float32
    )


def contract_first(left_rows, right_rows):
    return lax.dot_general(
        left_rows, right_rows, (((0,), (0,)), ((), ())), preferred_element_type=jnp.float32
    )


def take_slot(slot_store, slot_index):
    return lax.dynamic_index_in_dim(slot_store, slot_index, 0, keepdims=False)


def put_slot(slot_store, new_value, slot_index, active):
    previous = take_slot(slot_store, slot_index)
    return lax.dynamic_update_index_in_dim(
        slot_store, jnp.where(active, new_value, previous), slot_index, 0
    )


def local(
    hidden,
    unembed,
    value_proj,
    output_proj,
    norm_gains,
    survive,
    lengths,
    assign,
    advantage,
    reference_logit,
    recorded_gap,
):
    resp_count = hidden.shape[0]
    positions = hidden.shape[1]
    model_width = hidden.shape[2]
    half_value = value_proj.shape[2]
    micro_count = resp_count // MB_RESP
    row_count = MB_RESP * positions
    section_count = lax.axis_size("section")
    section_index = lax.axis_index("section")
    is_last = section_index == section_count - 1
    norm_gain = norm_gains[0]
    alive_mask = jnp.repeat(survive, GROUP)
    local_count = jnp.sum((alive_mask * lengths).astype(jnp.float32))
    gathered_value, gathered_output = turned_gather((value_proj, output_proj), "dp", (1, 2))
    w_first = gathered_value[0]
    w_second = gathered_output[0]

    def pick(array):
        return jnp.take(array, assign, axis=0, mode="fill", fill_value=0)

    slot_hidden = pick(hidden).reshape(micro_count, row_count, model_width)
    slot_unembed = pick(unembed).reshape(micro_count, row_count, model_width)
    position_index = lax.broadcasted_iota(jnp.int32, (resp_count, positions), 1)
    live_mask = (position_index < pick(lengths)[:, None]).astype(jnp.float32)
    advantages = jnp.broadcast_to(pick(advantage)[:, None], (resp_count, positions))
    gap_rows = pick(recorded_gap)
    clipped = (advantages > 0) & (gap_rows > clip_high) | (advantages < 0) & (gap_rows < clip_low)
    kept_mask = 1.0 - clipped.astype(jnp.float32)
    weight_rows = (-loss_scale * advantages * kept_mask * live_mask).reshape(micro_count, row_count)
    logit_base = pick(reference_logit).reshape(micro_count, row_count)
    step_count = micro_count + section_count - 1
    store_in = jnp.zeros((micro_count, row_count, model_width), jnp.bfloat16)
    store_normed = jnp.zeros((micro_count, row_count, model_width), jnp.bfloat16)
    store_projected = jnp.zeros((micro_count, row_count, half_value), jnp.bfloat16)
    store_out = jnp.zeros((micro_count, row_count, model_width), jnp.bfloat16)
    arriving = jnp.zeros((row_count, model_width), jnp.bfloat16)
    for step_index in range(step_count):
        micro_index = step_index - section_index
        active = (micro_index >= 0) & (micro_index < micro_count)
        clamped = jnp.clip(micro_index, 0, micro_count - 1)
        entering = jnp.where(section_index == 0, take_slot(slot_hidden, clamped), arriving)
        values, inverse, normed = norm_forward(entering, norm_gain)
        projected = jnp.dot(normed, w_first, preferred_element_type=jnp.float32).astype(
            jnp.bfloat16
        )
        partial_out = jnp.dot(projected, w_second, preferred_element_type=jnp.float32)
        mixed_sum = taken_together(partial_out.astype(jnp.bfloat16), "tensor").astype(jnp.float32)
        leaving = (values + mixed_sum).astype(jnp.bfloat16)
        store_in = put_slot(store_in, entering, clamped, active)
        store_normed = put_slot(store_normed, normed, clamped, active)
        store_projected = put_slot(store_projected, projected, clamped, active)
        store_out = put_slot(store_out, leaving, clamped, active)
        arriving = from_behind(leaving, "section", 1)
    store_upstream = jnp.zeros((micro_count, row_count, model_width), jnp.bfloat16)
    store_grad_value = jnp.zeros((micro_count, row_count, half_value), jnp.bfloat16)
    arriving = jnp.zeros((row_count, model_width), jnp.bfloat16)
    for step_index in range(step_count):
        micro_index = step_index - (section_count - 1 - section_index)
        active = (micro_index >= 0) & (micro_index < micro_count)
        clamped = jnp.clip(micro_index, 0, micro_count - 1)
        top_rows = take_slot(store_out, clamped).astype(jnp.float32)
        unembed_rows = take_slot(slot_unembed, clamped).astype(jnp.float32)
        logit = jnp.sum(top_rows * unembed_rows, axis=-1)
        seed_rows = take_slot(weight_rows, clamped) * jnp.exp(
            logit - take_slot(logit_base, clamped)
        )
        start_grad = (seed_rows[:, None] * unembed_rows).astype(jnp.bfloat16)
        upstream = jnp.where(is_last, start_grad, arriving)
        entering = take_slot(store_in, clamped)
        normed = take_slot(store_normed, clamped)
        projected = take_slot(store_projected, clamped)
        grad_projected = contract_last(upstream, w_second).astype(jnp.bfloat16)
        partial_norm = contract_last(grad_projected, w_first)
        grad_normed = taken_together(partial_norm.astype(jnp.bfloat16), "tensor").astype(
            jnp.float32
        )
        values, inverse, unused_normed = norm_forward(entering, norm_gain)
        grad_entering = (
            upstream.astype(jnp.float32) + norm_backward(values, inverse, norm_gain, grad_normed)
        ).astype(jnp.bfloat16)
        store_upstream = put_slot(store_upstream, upstream, clamped, active)
        store_grad_value = put_slot(store_grad_value, grad_projected, clamped, active)
        arriving = from_behind(grad_entering, "section", -1)
    flat_normed = store_normed.reshape(micro_count * row_count, model_width)
    flat_upstream = store_upstream.reshape(micro_count * row_count, model_width)
    flat_grad_value = store_grad_value.reshape(micro_count * row_count, half_value)
    flat_projected = store_projected.reshape(micro_count * row_count, half_value)
    reduced = lax.psum_scatter(
        jnp.concatenate(
            [
                contract_first(flat_normed, flat_grad_value),
                contract_first(flat_upstream, flat_projected),
            ],
            axis=1,
        ).astype(jnp.bfloat16),
        "dp",
        scatter_dimension=0,
        tiled=True,
    ).astype(jnp.float32)
    token_total = of_everyone(local_count, "dp")
    scaled_grads = reduced / token_total
    grad_value = scaled_grads[:, :half_value][None]
    grad_output = scaled_grads[:, half_value:].T[None]
    return (grad_value, grad_output)


def solution(mesh):
    placed = (
        P(("groups", "dp"), None, None),
        P(("groups", "dp"), None, None),
        P("section", "dp", "tensor"),
        P("section", "tensor", "dp"),
        P("section", None),
        P(("groups", "dp")),
        P(("groups", "dp")),
        P(("groups", "dp")),
        P(("groups", "dp")),
        P(("groups", "dp"), None),
        P(("groups", "dp"), None),
    )
    return jax.shard_map(
        local,
        mesh=mesh,
        in_specs=placed,
        out_specs=(
            P(("groups", "section"), "dp", "tensor"),
            P(("groups", "section"), "tensor", "dp"),
        ),
        check_vma=False,
    )
```

profile of v0, /device:TPU:34, one launch (start us, length us, event | category | flops | bytes accessed | tf_op | source)
XLA Modules:
  0.0 454.4 jit_solution(10710032838537592977)
XLA Ops:
  20.5 82.5 %all-gather.2.cloned.1.call-done = bf16[5120,512]{1,0:T(8,128)(2,1)} async-done(((bf16[320,512]{1,0:T(8,128)(2,1)}), bf16[5120,512]{1,0:T(8,128)(2,1)}) %all-gather.2.cloned.1.call-update) | async-done | bytes 5242896 | tf_op jit(solution)/shard_map/all_gather | solution.py:19
  108.4 4.9 %all_to_all.51 = bf16[2,64,5120]{2,1,0:T(8,128)(2,1)S(1)} all-to-all(bf16[2,64,5120]{2,1,0:T(8,128)(2,1)S(1)} %broadcast_in_dim.204), channel_id=1, replica_groups=mesh['groups'=2,'dp'=16,'section'=4,'tensor'=2] {'tensor'}, dimensions={0} | all-to-all | bytes 2621440 | tf_op jit(solution)/shard_map/all_to_all | solution.py:31
  113.7 3.8 collective-permute-start
  117.7 15.0 %collective-permute-done = bf16[64,5120]{1,0:T(8,128)(2,1)S(1)} collective-permute-done((bf16[64,5120]{1,0:T(8,128)(2,1)S(1)}, bf16[64,5120]{1,0:T(8,128)(2,1)S(1)}, u32[]{:S(2)}, u32[]{:S(2)}) %collective-permute-start) | collective-permute-done | bytes 655392 | tf_op jit(solution)/shard_map/ppermute | solution.py:43
  137.1 4.5 %all-to-all-start.1 = ((bf16[2,64,5120]{2,1,0:T(8,128)(2,1)}), bf16[2,64,5120]{2,1,0:T(8,128)(2,1)}, u32[]{:S(2)}, u32[]{:S(2)}) async-start(bf16[2,64,5120]{2,1,0:T(8,128)(2,1)} %broadcast_in_dim.206), calls=%async_computation.1 | async-start | bytes 2621440 | tf_op jit(solution)/shard_map/all_to_all | solution.py:31
  146.2 3.8 collective-permute-start.1
  150.2 15.0 %collective-permute-done.1 = bf16[64,5120]{1,0:T(8,128)(2,1)S(1)} collective-permute-done((bf16[64,5120]{1,0:T(8,128)(2,1)S(1)}, bf16[64,5120]{1,0:T(8,128)(2,1)S(1)}, u32[]{:S(2)}, u32[]{:S(2)}) %collective-permute-start.1) | collective-permute-done | bytes 655392 | tf_op jit(solution)/shard_map/ppermute | solution.py:43
  167.4 4.8 %all_to_all.52 = bf16[2,64,5120]{2,1,0:T(8,128)(2,1)S(1)} all-to-all(bf16[2,64,5120]{2,1,0:T(8,128)(2,1)S(1)} %broadcast_in_dim.208), channel_id=1, replica_groups=mesh['groups'=2,'dp'=16,'section'=4,'tensor'=2] {'tensor'}, dimensions={0} | all-to-all | bytes 2621440 | tf_op jit(solution)/shard_map/all_to_all | solution.py:31
  176.5 15.0 %collective-permute-done.2 = bf16[64,5120]{1,0:T(8,128)(2,1)S(1)} collective-permute-done((bf16[64,5120]{1,0:T(8,128)(2,1)S(1)}, bf16[64,5120]{1,0:T(8,128)(2,1)S(1)}, u32[]{:S(2)}, u32[]{:S(2)}) %collective-permute-start.2) | collective-permute-done | bytes 655392 | tf_op jit(solution)/shard_map/ppermute | solution.py:43
  193.8 4.8 %all_to_all.53 = bf16[2,64,5120]{2,1,0:T(8,128)(2,1)S(1)} all-to-all(bf16[2,64,5120]{2,1,0:T(8,128)(2,1)S(1)} %broadcast_in_dim.210), channel_id=1, replica_groups=mesh['groups'=2,'dp'=16,'section'=4,'tensor'=2] {'tensor'}, dimensions={0} | all-to-all | bytes 2621440 | tf_op jit(solution)/shard_map/all_to_all | solution.py:31
  199.1 3.8 collective-permute-start.3
  203.9 13.9 %collective-permute-done.3 = bf16[64,5120]{1,0:T(8,128)(2,1)S(1)} collective-permute-done((bf16[64,5120]{1,0:T(8,128)(2,1)S(1)}, bf16[64,5120]{1,0:T(8,128)(2,1)S(1)}, u32[]{:S(2)}, u32[]{:S(2)}) %collective-permute-start.3) | collective-permute-done | bytes 655392 | tf_op jit(solution)/shard_map/ppermute | solution.py:43
  223.9 4.6 %all-to-all-start.4 = ((bf16[2,64,5120]{2,1,0:T(8,128)(2,1)}), bf16[2,64,5120]{2,1,0:T(8,128)(2,1)}, u32[]{:S(2)}, u32[]{:S(2)}) async-start(bf16[2,64,5120]{2,1,0:T(8,128)(2,1)} %broadcast_in_dim.219), calls=%async_computation.4 | async-start | bytes 2621440 | tf_op jit(solution)/shard_map/all_to_all | solution.py:31
  244.7 4.8 %all_to_all.54 = bf16[2,64,5120]{2,1,0:T(8,128)(2,1)S(1)} all-to-all(bf16[2,64,5120]{2,1,0:T(8,128)(2,1)S(1)} %broadcast_in_dim.226), channel_id=1, replica_groups=mesh['groups'=2,'dp'=16,'section'=4,'tensor'=2] {'tensor'}, dimensions={0} | all-to-all | bytes 2621440 | tf_op jit(solution)/shard_map/all_to_all | solution.py:31
  254.6 16.2 %collective-permute-done.4 = bf16[64,5120]{1,0:T(8,128)(2,1)S(1)} collective-permute-done((bf16[64,5120]{1,0:T(8,128)(2,1)S(1)}, bf16[64,5120]{1,0:T(8,128)(2,1)S(1)}, u32[]{:S(2)}, u32[]{:S(2)}) %collective-permute-start.4) | collective-permute-done | bytes 655392 | tf_op jit(solution)/shard_map/ppermute | solution.py:43
  272.9 4.8 %all_to_all.55 = bf16[2,64,5120]{2,1,0:T(8,128)(2,1)S(1)} all-to-all(bf16[2,64,5120]{2,1,0:T(8,128)(2,1)S(1)} %broadcast_in_dim.228), channel_id=1, replica_groups=mesh['groups'=2,'dp'=16,'section'=4,'tensor'=2] {'tensor'}, dimensions={0} | all-to-all | bytes 2621440 | tf_op jit(solution)/shard_map/all_to_all | solution.py:31
  281.2 16.2 %collective-permute-done.5 = bf16[64,5120]{1,0:T(8,128)(2,1)S(1)} collective-permute-done((bf16[64,5120]{1,0:T(8,128)(2,1)S(1)}, bf16[64,5120]{1,0:T(8,128)(2,1)S(1)}, u32[]{:S(2)}, u32[]{:S(2)}) %collective-permute-start.5) | collective-permute-done | bytes 655392 | tf_op jit(solution)/shard_map/ppermute | solution.py:43
  299.4 4.8 %all_to_all.56 = bf16[2,64,5120]{2,1,0:T(8,128)(2,1)S(1)} all-to-all(bf16[2,64,5120]{2,1,0:T(8,128)(2,1)S(1)} %broadcast_in_dim.230), channel_id=1, replica_groups=mesh['groups'=2,'dp'=16,'section'=4,'tensor'=2] {'tensor'}, dimensions={0} | all-to-all | bytes 2621440 | tf_op jit(solution)/shard_map/all_to_all | solution.py:31
  307.5 16.4 %collective-permute-done.6 = bf16[64,5120]{1,0:T(8,128)(2,1)S(1)} collective-permute-done((bf16[64,5120]{1,0:T(8,128)(2,1)S(1)}, bf16[64,5120]{1,0:T(8,128)(2,1)S(1)}, u32[]{:S(2)}, u32[]{:S(2)}) %collective-permute-start.6) | collective-permute-done | bytes 655392 | tf_op jit(solution)/shard_map/ppermute | solution.py:43
  325.9 4.8 %all_to_all.57 = bf16[2,64,5120]{2,1,0:T(8,128)(2,1)S(1)} all-to-all(bf16[2,64,5120]{2,1,0:T(8,128)(2,1)S(1)} %broadcast_in_dim.232), channel_id=1, replica_groups=mesh['groups'=2,'dp'=16,'section'=4,'tensor'=2] {'tensor'}, dimensions={0} | all-to-all | bytes 2621440 | tf_op jit(solution)/shard_map/all_to_all | solution.py:31
  334.0 16.4 %collective-permute-done.7 = bf16[64,5120]{1,0:T(8,128)(2,1)S(1)} collective-permute-done((bf16[64,5120]{1,0:T(8,128)(2,1)S(1)}, bf16[64,5120]{1,0:T(8,128)(2,1)S(1)}, u32[]{:S(2)}, u32[]{:S(2)}) %collective-permute-start.7) | collective-permute-done | bytes 655392 | tf_op jit(solution)/shard_map/ppermute | solution.py:43
  357.3 7.9 %copy.34 = bf16[5120,512]{1,0:T(8,128)(2,1)} copy(bf16[5120,512]{0,1:T(8,128)(2,1)} %pad_maximum_fusion) | data formatting | bytes 10485760
  367.2 19.5 %all_to_all.58 = f32[16,1,1]{2,1,0:T(1,128)S(1)} all-to-all(f32[16,1,1]{2,1,0:T(1,128)S(1)} %broadcast_in_dim.243), channel_id=1, replica_groups=mesh['groups'=2,'dp'=16,'section'=4,'tensor'=2] {'dp'}, dimensions={0} | all-to-all | bytes 128 | tf_op jit(solution)/shard_map/all_to_all | solution.py:31
  387.3 56.4 %reduce-scatter.4.cloned.1.call-done = bf16[320,512]{1,0:T(8,128)(2,1)} async-done(((bf16[5120,512]{1,0:T(8,128)(2,1)}), bf16[320,512]{1,0:T(8,128)(2,1)}) %reduce-scatter.4.cloned.1.call-update) | async-done | bytes 327696
  (218 shorter events, 93.9 us)
Async XLA Ops:
  7.2 95.8 %all-gather.2.cloned.1.call-start = ((), (), s32[]{:S(2)}) async-start(), calls=%async_computation.11 | async-start | bytes 5570560 | tf_op jit(solution)/shard_map/all_gather | solution.py:19
  11.2 5.0 %copy-start.24 = (s32[16]{0:T(128)S(1)}, s32[16]{0:T(128)}, u32[]{:S(2)}) copy-start(s32[16]{0:T(128)} %param.22) | copy-start | bytes 196
  19.5 83.5 %copy-start.20 = (f32[1,5120]{1,0:T(1,128)S(1)}, f32[1,5120]{1,0:T(1,128)}, u32[]{:S(2)}) copy-start(f32[1,5120]{1,0:T(1,128)} %param.19) | copy-start | bytes 61444
  108.4 5.2 %copy-start.14 = (bf16[16,8,5120]{2,1,0:T(8,128)(2,1)S(1)}, bf16[16,8,5120]{2,1,0:T(8,128)(2,1)}, u32[]{:S(2)}) copy-start(bf16[16,8,5120]{2,1,0:T(8,128)(2,1)} %copy-done.13) | copy-start | bytes 3932164
  113.3 20.3 %slice-start = ((s8[5242880]{0:T(1024)(128)(4,1)}), s8[4194304]{0:T(1024)(128)(4,1)S(1)}, s32[]{:S(2)}) async-start(s8[5242880]{0:T(1024)(128)(4,1)} %bitcast.385), calls=%async_computation.13 | async-start | bytes 8388608
  113.7 19.0 %collective-permute-start = (bf16[64,5120]{1,0:T(8,128)(2,1)S(1)}, bf16[64,5120]{1,0:T(8,128)(2,1)S(1)}, u32[]{:S(2)}, u32[]{:S(2)}) collective-permute-start(bf16[64,5120]{1,0:T(8,128)(2,1)S(1)} %fusion.21), channel_id=1, source_target_pairs={{0,2},{2,4},{4,6},{1,3},{3,5},{5,7},{8,10},{10,12},{12,14},{9,11},... | collective-permute-start | bytes 1966088 | tf_op jit(solution)/shard_map/ppermute | solution.py:43
  117.7 16.0 %slice-start.1 = ((s8[5242880]{0:T(1024)(128)(4,1)}), s8[1048576]{0:T(1024)(128)(4,1)S(1)}, s32[]{:S(2)}) async-start(s8[5242880]{0:T(1024)(128)(4,1)} %bitcast.385), calls=%async_computation.14 | async-start | bytes 2097152
  137.1 7.0 %all-to-all-start.1 = ((bf16[2,64,5120]{2,1,0:T(8,128)(2,1)}), bf16[2,64,5120]{2,1,0:T(8,128)(2,1)}, u32[]{:S(2)}, u32[]{:S(2)}) async-start(bf16[2,64,5120]{2,1,0:T(8,128)(2,1)} %broadcast_in_dim.206), calls=%async_computation.1 | async-start | bytes 2621440 | tf_op jit(solution)/shard_map/all_to_all | solution.py:31
  141.6 24.1 %slice-start.2 = ((s8[5242880]{0:T(1024)(128)(4,1)}), s8[1048576]{0:T(1024)(128)(4,1)S(1)}, s32[]{:S(2)}) async-start(s8[5242880]{0:T(1024)(128)(4,1)} %bitcast.387), calls=%async_computation.15 | async-start | bytes 2097152
  144.0 6.0 %copy-start.5 = (bf16[2,64,5120]{2,1,0:T(8,128)(2,1)S(1)}, bf16[2,64,5120]{2,1,0:T(8,128)(2,1)}, u32[]{:S(2)}) copy-start(bf16[2,64,5120]{2,1,0:T(8,128)(2,1)} %copy-done.4) | copy-start | bytes 3932164
  145.9 19.9 %slice-start.3 = ((s8[5242880]{0:T(1024)(128)(4,1)}), s8[4194304]{0:T(1024)(128)(4,1)S(1)}, s32[]{:S(2)}) async-start(s8[5242880]{0:T(1024)(128)(4,1)} %bitcast.387), calls=%async_computation.16 | async-start | bytes 8388608
  146.2 19.0 %collective-permute-start.1 = (bf16[64,5120]{1,0:T(8,128)(2,1)S(1)}, bf16[64,5120]{1,0:T(8,128)(2,1)S(1)}, u32[]{:S(2)}, u32[]{:S(2)}) collective-permute-start(bf16[64,5120]{1,0:T(8,128)(2,1)S(1)} %get-tuple-element.43), channel_id=1, source_target_pairs={{0,2},{2,4},{4,6},{1,3},{3,5},{5,7},{8,10},{10,12},{12,14},{9,11},... | collective-permute-start | bytes 1966088 | tf_op jit(solution)/shard_map/ppermute | solution.py:43
  150.1 15.1 %copy-start.15 = (bf16[16,8,5120]{2,1,0:T(8,128)(2,1)S(1)}, bf16[16,8,5120]{2,1,0:T(8,128)(2,1)}, u32[]{:S(2)}) copy-start(bf16[16,8,5120]{2,1,0:T(8,128)(2,1)} %copy-done.13) | copy-start | bytes 3932164
  172.8 18.7 %collective-permute-start.2 = (bf16[64,5120]{1,0:T(8,128)(2,1)S(1)}, bf16[64,5120]{1,0:T(8,128)(2,1)S(1)}, u32[]{:S(2)}, u32[]{:S(2)}) collective-permute-start(bf16[64,5120]{1,0:T(8,128)(2,1)S(1)} %get-tuple-element.41), channel_id=1, source_target_pairs={{0,2},{2,4},{4,6},{1,3},{3,5},{5,7},{8,10},{10,12},{12,14},{9,11},... | collective-permute-start | bytes 1966088 | tf_op jit(solution)/shard_map/ppermute | solution.py:43
  191.8 7.0 %copy-start.16 = (bf16[64,5120]{1,0:T(8,128)(2,1)}, bf16[64,5120]{1,0:T(8,128)(2,1)S(1)}, u32[]{:S(2)}) copy-start(bf16[64,5120]{1,0:T(8,128)(2,1)S(1)} %get-tuple-element.33) | copy-start | bytes 1966084
  199.1 18.7 %collective-permute-start.3 = (bf16[64,5120]{1,0:T(8,128)(2,1)S(1)}, bf16[64,5120]{1,0:T(8,128)(2,1)S(1)}, u32[]{:S(2)}, u32[]{:S(2)}) collective-permute-start(bf16[64,5120]{1,0:T(8,128)(2,1)S(1)} %get-tuple-element.39), channel_id=1, source_target_pairs={{0,2},{2,4},{4,6},{1,3},{3,5},{5,7},{8,10},{10,12},{12,14},{9,11},... | collective-permute-start | bytes 1966088 | tf_op jit(solution)/shard_map/ppermute | solution.py:43
  223.9 13.7 %all-to-all-start.4 = ((bf16[2,64,5120]{2,1,0:T(8,128)(2,1)}), bf16[2,64,5120]{2,1,0:T(8,128)(2,1)}, u32[]{:S(2)}, u32[]{:S(2)}) async-start(bf16[2,64,5120]{2,1,0:T(8,128)(2,1)} %broadcast_in_dim.219), calls=%async_computation.4 | async-start | bytes 2621440 | tf_op jit(solution)/shard_map/all_to_all | solution.py:31
  228.4 215.2 %reduce-scatter.4.cloned.1.call-start = ((), (), s32[]{:S(2)}) async-start(), calls=%async_computation.12 | async-start | bytes 5570560
  234.3 5.1 %copy-start.21 = (bf16[1,64,5120]{2,1,0:T(8,128)(2,1)S(1)}, bf16[1,64,5120]{2,1,0:T(8,128)(2,1)}, u32[]{:S(2)}) copy-start(bf16[1,64,5120]{2,1,0:T(8,128)(2,1)} %constant_dynamic-slice_fusion.25) | copy-start | bytes 1966084
  237.5 5.5 %slice-start.4 = ((s8[5242880]{0:T(1024)(128)(4,1)}), s8[4194304]{0:T(1024)(128)(4,1)S(1)}, s32[]{:S(2)}) async-start(s8[5242880]{0:T(1024)(128)(4,1)} %bitcast.389), calls=%async_computation.17 | async-start | bytes 8388608
  252.2 18.7 %collective-permute-start.4 = (bf16[64,5120]{1,0:T(8,128)(2,1)S(1)}, bf16[64,5120]{1,0:T(8,128)(2,1)S(1)}, u32[]{:S(2)}, u32[]{:S(2)}) collective-permute-start(bf16[64,5120]{1,0:T(8,128)(2,1)S(1)} %fusion.45), channel_id=1, source_target_pairs={{2,0},{4,2},{6,4},{3,1},{5,3},{7,5},{10,8},{12,10},{14,12},{11,9},... | collective-permute-start | bytes 1966088 | tf_op jit(solution)/shard_map/ppermute | solution.py:43
  278.7 18.7 %collective-permute-start.5 = (bf16[64,5120]{1,0:T(8,128)(2,1)S(1)}, bf16[64,5120]{1,0:T(8,128)(2,1)S(1)}, u32[]{:S(2)}, u32[]{:S(2)}) collective-permute-start(bf16[64,5120]{1,0:T(8,128)(2,1)S(1)} %fusion.51), channel_id=1, source_target_pairs={{2,0},{4,2},{6,4},{3,1},{5,3},{7,5},{10,8},{12,10},{14,12},{11,9},... | collective-permute-start | bytes 1966088 | tf_op jit(solution)/shard_map/ppermute | solution.py:43
  305.2 18.7 %collective-permute-start.6 = (bf16[64,5120]{1,0:T(8,128)(2,1)S(1)}, bf16[64,5120]{1,0:T(8,128)(2,1)S(1)}, u32[]{:S(2)}, u32[]{:S(2)}) collective-permute-start(bf16[64,5120]{1,0:T(8,128)(2,1)S(1)} %fusion.57), channel_id=1, source_target_pairs={{2,0},{4,2},{6,4},{3,1},{5,3},{7,5},{10,8},{12,10},{14,12},{11,9},... | collective-permute-start | bytes 1966088 | tf_op jit(solution)/shard_map/ppermute | solution.py:43
  331.7 18.7 %collective-permute-start.7 = (bf16[64,5120]{1,0:T(8,128)(2,1)S(1)}, bf16[64,5120]{1,0:T(8,128)(2,1)S(1)}, u32[]{:S(2)}, u32[]{:S(2)}) collective-permute-start(bf16[64,5120]{1,0:T(8,128)(2,1)S(1)} %fusion.63), channel_id=1, source_target_pairs={{2,0},{4,2},{6,4},{3,1},{5,3},{7,5},{10,8},{12,10},{14,12},{11,9},... | collective-permute-start | bytes 1966088 | tf_op jit(solution)/shard_map/ppermute | solution.py:43
  (19 other events, 48.4 us)
Sparse Core Ops, SparseCore 0:
  10.4 92.5 all-gather.1
  365.4 78.2 reduce-scatter.3
where the time goes:
time: 456 us; the launch traced here: 454 us
  waiting for transfers between devices  264 us (58%)
  blocking collectives  53.2 us (12%)
  local copies, waits for them, and re-layouts  34.1 us (7%)
  starting transfers between devices  33.1 us (7%)
  other arithmetic  33 us (7%)
  matrix products  20.9 us (5%)
  between operations  15.8 us (3%)
    ppermute x8, waiting for transfers between devices, from_behind(): return lax.ppermute(block, axis, route)  124 us
    all_gather x1, waiting for transfers between devices, turned_gather(): result = lax.all_gather(both, axis, axis=0, tiled=True)  82.5 us
    unnamed x3, waiting for transfers between devices  56.5 us
    all_to_all x8, blocking collectives, copy_for_each(): lax.all_to_all(jnp.broadcast_to(array[None], (devices, *array.shape)), ax...  53.2 us
    ppermute x8, starting transfers between devices, from_behind(): return lax.ppermute(block, axis, route)  23.9 us
    unnamed x68, local copies, waits for them, and re-layouts  13.9 us
    dynamic_update_slice x17, other arithmetic, put_slot(): lax.dynamic_update_index_in_dim(slot_store, jnp.where(active, new_value,...  11.7 us
    all_to_all x2, starting transfers between devices, copy_for_each(): lax.all_to_all(jnp.broadcast_to(array[None], (devices, *array.shape)), ax...  9.13 us
  transfers between devices with their start and end apart: 12, of which 11 were waited for; matrix products, arithmetic and copies ran while one was open for 5% of the time, Pallas kernels for 0%

commit v1 on v0

--- a/solution.py
+++ b/solution.py
@@ -16,7 +16,9 @@
     turned = [jnp.moveaxis(a, dim, 0) for a, dim in zip(arrays, dims)]
     widths = [t[0].size for t in turned]
     both = jnp.concatenate([t.reshape(-1, w) for t, w in zip(turned, widths)], axis=1)
-    result = lax.all_gather(both, axis, axis=0, tiled=True)
+    result = jnp.concatenate(
+        lax.all_to_all(jnp.stack([both] * lax.axis_size(axis)), axis, 0, 0), axis=0
+    )
     tiles = jnp.split(result, [sum(widths[:k]) for k in range(1, len(widths))], axis=1)
     return tuple(
         (

time: 456 us -> 649 us (1.42)
  waiting for transfers between devices: 264 us -> 400 us
  matrix products: 20.9 us -> 50.9 us
  starting transfers between devices: 33.1 us -> 56.5 us
    all_to_all x0 -> x1, waiting for transfers between devices: none -> 218 us  [turned_gather(): lax.all_to_all(jnp.stack([both] * lax.axis_size(axis)), axis, 0, 0)]
    all_gather x1 -> x0, waiting for transfers between devices: 82.5 us -> none  [turned_gather(): result = lax.all_gather(both, axis, axis=0, tiled=True)]
    all_to_all x0 -> x1, starting transfers between devices: none -> 24.1 us  [turned_gather(): lax.all_to_all(jnp.stack([both] * lax.axis_size(axis)), axis, 0, 0)]
    dot_general x9, matrix products: 6.51 us -> 22.3 us  [contract_last(): lax.dot_general(left_rows, right_rows, (((1,), (1,)), ((), ())), preferre...]
    dot_general x5, matrix products: 5.08 us -> 12.3 us  [local(): jnp.dot(normed, w_first, preferred_element_type=jnp.float32)]
    dot_general x5, matrix products: 6.27 us -> 13.2 us  [local(): jnp.dot(projected, w_second, preferred_element_type=jnp.float32)]
    unnamed x3 -> x2, waiting for transfers between devices: 56.5 us -> 57.5 us
    unnamed x68 -> x56, local copies, waits for them, and re-layouts: 13.9 us -> 13.1 us
  transfers between devices with their start and end apart: 12 -> 12, of which waited for: 11 -> 11; matrix products, arithmetic and copies ran while one was open for 5% -> 4% of each run, Pallas kernels for 0% -> 0%
where the time goes in v1:
time: 649 us; the launch traced here: 647 us
  waiting for transfers between devices  400 us (62%)
  blocking collectives  56.7 us (9%)
  starting transfers between devices  56.5 us (9%)
  matrix products  50.9 us (8%)
  local copies, waits for them, and re-layouts  36.6 us (6%)
  other arithmetic  30.4 us (5%)
  between operations  15.7 us (2%)
    all_to_all x1, waiting for transfers between devices, turned_gather(): lax.all_to_all(jnp.stack([both] * lax.axis_size(axis)), axis, 0, 0)  218 us
    ppermute x8, waiting for transfers between devices, from_behind(): return lax.ppermute(block, axis, route)  124 us
    unnamed x2, waiting for transfers between devices  57.5 us
    all_to_all x8, blocking collectives, copy_for_each(): lax.all_to_all(jnp.broadcast_to(array[None], (devices, *array.shape)), ax...  56.7 us
    all_to_all x1, starting transfers between devices, turned_gather(): lax.all_to_all(jnp.stack([both] * lax.axis_size(axis)), axis, 0, 0)  24.1 us
    ppermute x8, starting transfers between devices, from_behind(): return lax.ppermute(block, axis, route)  23.3 us
    dot_general x9, matrix products, contract_last(): lax.dot_general(left_rows, right_rows, (((1,), (1,)), ((), ())), preferre...  22.3 us
    dot_general x5, matrix products, local(): jnp.dot(projected, w_second, preferred_element_type=jnp.float32)  13.2 us
  transfers between devices with their start and end apart: 12, of which 11 were waited for; matrix products, arithmetic and copies ran while one was open for 4% of the time, Pallas kernels for 0%

profile of v1, /device:TPU:34, one launch (start us, length us, event | category | flops | bytes accessed | tf_op | source)
XLA Modules:
  0.0 646.7 jit_solution(6820810458116784555)
XLA Ops:
  11.2 24.1 %all-to-all-start = ((bf16[16,320,512]{2,1,0:T(8,128)(2,1)}), bf16[16,320,512]{2,1,0:T(8,128)(2,1)}, u32[]{:S(2)}, u32[]{:S(2)}) async-start(bf16[16,320,512]{2,1,0:T(8,128)(2,1)} %stack.2), calls=%async_computation | async-start | bytes 10485760 | tf_op jit(solution)/shard_map/all_to_all | solution.py:20
  44.6 217.8 %all-to-all-done = bf16[16,320,512]{2,1,0:T(8,128)(2,1)} async-done(((bf16[16,320,512]{2,1,0:T(8,128)(2,1)}), bf16[16,320,512]{2,1,0:T(8,128)(2,1)}, u32[]{:S(2)}, u32[]{:S(2)}) %all-to-all-start) | async-done | bytes 5242912 | tf_op jit(solution)/shard_map/all_to_all | solution.py:20
  267.8 4.8 all_to_all.56
  274.1 3.6 collective-permute-start
  277.8 15.0 %collective-permute-done = bf16[64,5120]{1,0:T(8,128)(2,1)S(1)} collective-permute-done((bf16[64,5120]{1,0:T(8,128)(2,1)S(1)}, bf16[64,5120]{1,0:T(8,128)(2,1)S(1)}, u32[]{:S(2)}, u32[]{:S(2)}) %collective-permute-start) | collective-permute-done | bytes 655392 | tf_op jit(solution)/shard_map/ppermute | solution.py:45
  300.3 4.5 all-to-all-start.2
  313.1 15.0 %collective-permute-done.1 = bf16[64,5120]{1,0:T(8,128)(2,1)S(1)} collective-permute-done((bf16[64,5120]{1,0:T(8,128)(2,1)S(1)}, bf16[64,5120]{1,0:T(8,128)(2,1)S(1)}, u32[]{:S(2)}, u32[]{:S(2)}) %collective-permute-start.1) | collective-permute-done | bytes 655392 | tf_op jit(solution)/shard_map/ppermute | solution.py:45
  333.9 4.8 all_to_all.57
  343.0 15.0 %collective-permute-done.2 = bf16[64,5120]{1,0:T(8,128)(2,1)S(1)} collective-permute-done((bf16[64,5120]{1,0:T(8,128)(2,1)S(1)}, bf16[64,5120]{1,0:T(8,128)(2,1)S(1)}, u32[]{:S(2)}, u32[]{:S(2)}) %collective-permute-start.2) | collective-permute-done | bytes 655392 | tf_op jit(solution)/shard_map/ppermute | solution.py:45
  363.7 4.8 all_to_all.58
  369.1 3.7 collective-permute-start.3
  373.8 14.0 %collective-permute-done.3 = bf16[64,5120]{1,0:T(8,128)(2,1)S(1)} collective-permute-done((bf16[64,5120]{1,0:T(8,128)(2,1)S(1)}, bf16[64,5120]{1,0:T(8,128)(2,1)S(1)}, u32[]{:S(2)}, u32[]{:S(2)}) %collective-permute-start.3) | collective-permute-done | bytes 655392 | tf_op jit(solution)/shard_map/ppermute | solution.py:45
  397.0 4.5 all-to-all-start.5
  421.2 4.8 all_to_all.59
  430.1 16.2 %collective-permute-done.4 = bf16[64,5120]{1,0:T(8,128)(2,1)S(1)} collective-permute-done((bf16[64,5120]{1,0:T(8,128)(2,1)S(1)}, bf16[64,5120]{1,0:T(8,128)(2,1)S(1)}, u32[]{:S(2)}, u32[]{:S(2)}) %collective-permute-start.4) | collective-permute-done | bytes 655392 | tf_op jit(solution)/shard_map/ppermute | solution.py:45
  451.8 4.8 all_to_all.60
  460.1 16.2 %collective-permute-done.5 = bf16[64,5120]{1,0:T(8,128)(2,1)S(1)} collective-permute-done((bf16[64,5120]{1,0:T(8,128)(2,1)S(1)}, bf16[64,5120]{1,0:T(8,128)(2,1)S(1)}, u32[]{:S(2)}, u32[]{:S(2)}) %collective-permute-start.5) | collective-permute-done | bytes 655392 | tf_op jit(solution)/shard_map/ppermute | solution.py:45
  481.8 4.8 all_to_all.61
  489.9 16.4 %collective-permute-done.6 = bf16[64,5120]{1,0:T(8,128)(2,1)S(1)} collective-permute-done((bf16[64,5120]{1,0:T(8,128)(2,1)S(1)}, bf16[64,5120]{1,0:T(8,128)(2,1)S(1)}, u32[]{:S(2)}, u32[]{:S(2)}) %collective-permute-start.6) | collective-permute-done | bytes 655392 | tf_op jit(solution)/shard_map/ppermute | solution.py:45
  511.8 4.8 all_to_all.62
  519.9 16.4 %collective-permute-done.7 = bf16[64,5120]{1,0:T(8,128)(2,1)S(1)} collective-permute-done((bf16[64,5120]{1,0:T(8,128)(2,1)S(1)}, bf16[64,5120]{1,0:T(8,128)(2,1)S(1)}, u32[]{:S(2)}, u32[]{:S(2)}) %collective-permute-start.7) | collective-permute-done | bytes 655392 | tf_op jit(solution)/shard_map/ppermute | solution.py:45
  545.0 7.9 %copy.34 = bf16[5120,512]{1,0:T(8,128)(2,1)} copy(bf16[5120,512]{0,1:T(8,128)(2,1)} %pad_maximum_fusion) | data formatting | bytes 10485760
  554.9 23.1 %all_to_all.63 = f32[16,1,1]{2,1,0:T(1,128)S(1)} all-to-all(f32[16,1,1]{2,1,0:T(1,128)S(1)} %broadcast_in_dim.243), channel_id=1, replica_groups=mesh['groups'=2,'dp'=16,'section'=4,'tensor'=2] {'dp'}, dimensions={0} | all-to-all | bytes 128 | tf_op jit(solution)/shard_map/all_to_all | solution.py:33
  578.6 57.5 %reduce-scatter.4.cloned.1.call-done = bf16[320,512]{1,0:T(8,128)(2,1)} async-done(((bf16[5120,512]{1,0:T(8,128)(2,1)}), bf16[320,512]{1,0:T(8,128)(2,1)}) %reduce-scatter.4.cloned.1.call-update) | async-done | bytes 327696
  (203 shorter events, 126.5 us)
Async XLA Ops:
  7.2 28.9 %copy-start = (bf16[16,8,5120]{2,1,0:T(8,128)(2,1)S(1)}, bf16[16,8,5120]{2,1,0:T(8,128)(2,1)}, u32[]{:S(2)}) copy-start(bf16[16,8,5120]{2,1,0:T(8,128)(2,1)} %param.15) | copy-start | bytes 3932164
  11.2 24.2 %copy-start.24 = (s32[16]{0:T(128)S(1)}, s32[16]{0:T(128)}, u32[]{:S(2)}) copy-start(s32[16]{0:T(128)} %param.22) | copy-start | bytes 196
  11.2 24.2 %copy-start.2 = (f32[16]{0:T(128)S(1)}, f32[16]{0:T(128)}, u32[]{:S(2)}) copy-start(f32[16]{0:T(128)} %param.23) | copy-start | bytes 196
  11.2 251.3 %all-to-all-start = ((bf16[16,320,512]{2,1,0:T(8,128)(2,1)}), bf16[16,320,512]{2,1,0:T(8,128)(2,1)}, u32[]{:S(2)}, u32[]{:S(2)}) async-start(bf16[16,320,512]{2,1,0:T(8,128)(2,1)} %stack.2), calls=%async_computation | async-start | bytes 10485760 | tf_op jit(solution)/shard_map/all_to_all | solution.py:20
  37.8 3.1 copy-start.23
  37.8 4.0 copy-start.17
  43.7 218.8 %copy-start.18 = (f32[1,5120]{1,0:T(1,128)S(1)}, f32[1,5120]{1,0:T(1,128)}, u32[]{:S(2)}) copy-start(f32[1,5120]{1,0:T(1,128)} %param.19) | copy-start | bytes 61444
  274.1 18.7 %collective-permute-start = (bf16[64,5120]{1,0:T(8,128)(2,1)S(1)}, bf16[64,5120]{1,0:T(8,128)(2,1)S(1)}, u32[]{:S(2)}, u32[]{:S(2)}) collective-permute-start(bf16[64,5120]{1,0:T(8,128)(2,1)S(1)} %fusion.21), channel_id=1, source_target_pairs={{0,2},{2,4},{4,6},{1,3},{3,5},{5,7},{8,10},{10,12},{12,14},{9,11},... | collective-permute-start | bytes 1966088 | tf_op jit(solution)/shard_map/ppermute | solution.py:45
  293.5 5.5 copy-start.4
  300.3 7.0 %all-to-all-start.2 = ((bf16[2,64,5120]{2,1,0:T(8,128)(2,1)}), bf16[2,64,5120]{2,1,0:T(8,128)(2,1)}, u32[]{:S(2)}, u32[]{:S(2)}) async-start(bf16[2,64,5120]{2,1,0:T(8,128)(2,1)} %broadcast_in_dim.206), calls=%async_computation.2 | async-start | bytes 2621440 | tf_op jit(solution)/shard_map/all_to_all | solution.py:33
  309.4 18.7 %collective-permute-start.1 = (bf16[64,5120]{1,0:T(8,128)(2,1)S(1)}, bf16[64,5120]{1,0:T(8,128)(2,1)S(1)}, u32[]{:S(2)}, u32[]{:S(2)}) collective-permute-start(bf16[64,5120]{1,0:T(8,128)(2,1)S(1)} %get-tuple-element.43), channel_id=1, source_target_pairs={{0,2},{2,4},{4,6},{1,3},{3,5},{5,7},{8,10},{10,12},{12,14},{9,11},... | collective-permute-start | bytes 1966088 | tf_op jit(solution)/shard_map/ppermute | solution.py:45
  313.0 15.1 %copy-start.10 = (bf16[16,8,5120]{2,1,0:T(8,128)(2,1)S(1)}, bf16[16,8,5120]{2,1,0:T(8,128)(2,1)}, u32[]{:S(2)}) copy-start(bf16[16,8,5120]{2,1,0:T(8,128)(2,1)} %copy-done.8) | copy-start | bytes 3932164
  328.4 10.5 %copy-start.11 = (bf16[64,5120]{1,0:T(8,128)(2,1)}, bf16[64,5120]{1,0:T(8,128)(2,1)S(1)}, u32[]{:S(2)}) copy-start(bf16[64,5120]{1,0:T(8,128)(2,1)S(1)} %get-tuple-element.35) | copy-start | bytes 1966084
  339.2 18.7 %collective-permute-start.2 = (bf16[64,5120]{1,0:T(8,128)(2,1)S(1)}, bf16[64,5120]{1,0:T(8,128)(2,1)S(1)}, u32[]{:S(2)}, u32[]{:S(2)}) collective-permute-start(bf16[64,5120]{1,0:T(8,128)(2,1)S(1)} %get-tuple-element.41), channel_id=1, source_target_pairs={{0,2},{2,4},{4,6},{1,3},{3,5},{5,7},{8,10},{10,12},{12,14},{9,11},... | collective-permute-start | bytes 1966088 | tf_op jit(solution)/shard_map/ppermute | solution.py:45
  358.3 10.5 %copy-start.13 = (bf16[64,5120]{1,0:T(8,128)(2,1)}, bf16[64,5120]{1,0:T(8,128)(2,1)S(1)}, u32[]{:S(2)}) copy-start(bf16[64,5120]{1,0:T(8,128)(2,1)S(1)} %get-tuple-element.33) | copy-start | bytes 1966084
  369.1 21.3 %copy-start.6 = (bf16[2,64,5120]{2,1,0:T(8,128)(2,1)}, bf16[2,64,5120]{2,1,0:T(8,128)(2,1)S(1)}, u32[]{:S(2)}) copy-start(bf16[2,64,5120]{2,1,0:T(8,128)(2,1)S(1)} %get-tuple-element.38) | copy-start | bytes 3932164
  369.1 18.7 %collective-permute-start.3 = (bf16[64,5120]{1,0:T(8,128)(2,1)S(1)}, bf16[64,5120]{1,0:T(8,128)(2,1)S(1)}, u32[]{:S(2)}, u32[]{:S(2)}) collective-permute-start(bf16[64,5120]{1,0:T(8,128)(2,1)S(1)} %get-tuple-element.39), channel_id=1, source_target_pairs={{0,2},{2,4},{4,6},{1,3},{3,5},{5,7},{8,10},{10,12},{12,14},{9,11},... | collective-permute-start | bytes 1966088 | tf_op jit(solution)/shard_map/ppermute | solution.py:45
  397.0 13.5 %all-to-all-start.5 = ((bf16[2,64,5120]{2,1,0:T(8,128)(2,1)}), bf16[2,64,5120]{2,1,0:T(8,128)(2,1)}, u32[]{:S(2)}, u32[]{:S(2)}) async-start(bf16[2,64,5120]{2,1,0:T(8,128)(2,1)} %broadcast_in_dim.219), calls=%async_computation.5 | async-start | bytes 2621440 | tf_op jit(solution)/shard_map/all_to_all | solution.py:33
  401.5 234.5 %reduce-scatter.4.cloned.1.call-start = ((), (), s32[]{:S(2)}) async-start(), calls=%async_computation.12 | async-start | bytes 5570560
  427.6 18.7 %collective-permute-start.4 = (bf16[64,5120]{1,0:T(8,128)(2,1)S(1)}, bf16[64,5120]{1,0:T(8,128)(2,1)S(1)}, u32[]{:S(2)}, u32[]{:S(2)}) collective-permute-start(bf16[64,5120]{1,0:T(8,128)(2,1)S(1)} %fusion.45), channel_id=1, source_target_pairs={{2,0},{4,2},{6,4},{3,1},{5,3},{7,5},{10,8},{12,10},{14,12},{11,9},... | collective-permute-start | bytes 1966088 | tf_op jit(solution)/shard_map/ppermute | solution.py:45
  457.6 18.7 %collective-permute-start.5 = (bf16[64,5120]{1,0:T(8,128)(2,1)S(1)}, bf16[64,5120]{1,0:T(8,128)(2,1)S(1)}, u32[]{:S(2)}, u32[]{:S(2)}) collective-permute-start(bf16[64,5120]{1,0:T(8,128)(2,1)S(1)} %fusion.51), channel_id=1, source_target_pairs={{2,0},{4,2},{6,4},{3,1},{5,3},{7,5},{10,8},{12,10},{14,12},{11,9},... | collective-permute-start | bytes 1966088 | tf_op jit(solution)/shard_map/ppermute | solution.py:45
  487.6 18.7 %collective-permute-start.6 = (bf16[64,5120]{1,0:T(8,128)(2,1)S(1)}, bf16[64,5120]{1,0:T(8,128)(2,1)S(1)}, u32[]{:S(2)}, u32[]{:S(2)}) collective-permute-start(bf16[64,5120]{1,0:T(8,128)(2,1)S(1)} %fusion.57), channel_id=1, source_target_pairs={{2,0},{4,2},{6,4},{3,1},{5,3},{7,5},{10,8},{12,10},{14,12},{11,9},... | collective-permute-start | bytes 1966088 | tf_op jit(solution)/shard_map/ppermute | solution.py:45
  517.6 18.7 %collective-permute-start.7 = (bf16[64,5120]{1,0:T(8,128)(2,1)S(1)}, bf16[64,5120]{1,0:T(8,128)(2,1)S(1)}, u32[]{:S(2)}, u32[]{:S(2)}) collective-permute-start(bf16[64,5120]{1,0:T(8,128)(2,1)S(1)} %fusion.63), channel_id=1, source_target_pairs={{2,0},{4,2},{6,4},{3,1},{5,3},{7,5},{10,8},{12,10},{14,12},{11,9},... | collective-permute-start | bytes 1966088 | tf_op jit(solution)/shard_map/ppermute | solution.py:45
  637.2 2.6 copy-start.1
  (13 other events, 25.1 us)
Sparse Core Ops, SparseCore 0:
  553.1 82.9 reduce-scatter.3
